TPU v7x, 32 devices: a whole 2x2x4 slice. The times are simulated.
32 devices in a mesh: dp: 8 (over z, y), sy: 2 (over x), sx: 2 (over core).
Axes of the slice: x: 2, y: 2, z: 4, core: 2. Of those that a mesh axis runs over, the one named last changes fastest.
Arguments:
- features: bfloat16 [8, 56, 56, 256], P('dp', 'sy', 'sx'), may hold values from -8 to 8
- labels: int32 [8], P('dp'), may hold values from 0 to 999
- grid: int32 [2], replicated, may hold values from 0 to 49
- w_reduce: bfloat16 [3, 256, 64], P(None, None, 'dp'), may hold values from -0.375 to 0.375
- w_spatial: bfloat16 [3, 3, 3, 64, 64], P(None, None, None, None, 'dp'), may hold values from -0.25 to 0.25
- w_expand: bfloat16 [3, 64, 256], P(None, None, 'dp'), may hold values from -0.75 to 0.75
- w_class: bfloat16 [256, 1000], P('dp'), may hold values from -1.5 to 1.5
- dir_reduce: bfloat16 [2, 3, 256, 64], P(None, None, None, 'dp'), may hold values from -6 to 6
- dir_spatial: bfloat16 [2, 3, 3, 3, 64, 64], P(None, None, None, None, None, 'dp'), may hold values from -6 to 6
- dir_expand: bfloat16 [2, 3, 64, 256], P(None, None, None, 'dp'), may hold values from -6 to 6
- dir_class: bfloat16 [2, 256, 1000], P(None, 'dp'), may hold values from -6 to 6
- gain_mid: float32 [3, 2, 64], replicated, may hold values from 0.5 to 1.5
- shift_mid: float32 [3, 2, 64], replicated, may hold values from -3 to 3
- gain_out: float32 [3, 256], replicated, may hold values from 0.5 to 1.5
- shift_out: float32 [3, 256], replicated, may hold values from -3 to 3
Outputs:
- section_out: bfloat16 [8, 56, 56, 256], P('dp', 'sy', 'sx')
- image_loss: float32 [8], P('dp')
- mean_loss: float32 [], replicated
All inputs are finite; a program needn't handle non-finite values.
Results may differ from a plain program's by a relative error of at most 0.012.
Values may be sent and summed in bfloat16 or wider, within the bound.
A program may use at most 64 MiB of HBM per device.

v0:
```python
import jax
import jax.numpy as jnp
from jax import lax
from jax.sharding import PartitionSpec as P

BLOCKS = 3
GRID = 50


EPS_NORM = 1e-06
EPS_BN = 1e-05


def extended(cells, sides, width):
    for axis, dim in sides:
        count = lax.axis_size(axis)
        ends = count - 1
        head = lax.slice_in_dim(cells, 0, width, axis=dim)
        tail = lax.slice_in_dim(cells, cells.shape[dim] - width, cells.shape[dim], axis=dim)
        cells = jnp.concatenate(
            [
                lax.ppermute(tail, axis, [(i, (i + 1) % count) for i in range(ends)]),
                cells,
                lax.ppermute(head, axis, [((i + 1) % count, i) for i in range(ends)]),
            ],
            axis=dim,
        )
    return cells


def coefficients(grid):
    values = grid.astype(jnp.float32)
    alpha = (2.0 * values + 1.0 - GRID) / GRID
    return (alpha[0], alpha[1])


def filter_ratio(base, direction):
    base_norm = jnp.sqrt(jnp.sum(jnp.square(base.astype(jnp.float32)), axis=0, keepdims=True))
    dir_norm = jnp.sqrt(
        jnp.sum(jnp.square(direction.astype(jnp.float32)), axis=0, keepdims=True) + EPS_NORM
    )
    return base_norm / dir_norm


def combine_filters(base, dir_a, dir_b, alpha_a, alpha_b):
    ratio_a = filter_ratio(base, dir_a)
    ratio_b = filter_ratio(base, dir_b)
    value = (
        base.astype(jnp.float32)
        + alpha_a * ratio_a * dir_a.astype(jnp.float32)
        + alpha_b * ratio_b * dir_b.astype(jnp.float32)
    )
    return value.astype(jnp.bfloat16)


def perturbed_product(left, base, dir_a, dir_b, alpha_a, alpha_b):
    local = combine_filters(base, dir_a, dir_b, alpha_a, alpha_b)
    return jnp.dot(
        left, lax.all_gather(local, "dp", axis=1, tiled=True), preferred_element_type=jnp.float32
    )


def normalize(y, gain, shift, count):
    mean = lax.psum(jnp.sum(y, axis=0), ("dp", "sy", "sx")) / count
    centred = y - mean
    var = lax.psum(jnp.sum(centred * centred, axis=0), ("dp", "sy", "sx")) / count
    return centred * lax.rsqrt(var + EPS_BN) * gain + shift


def padded_tile(inner):
    return extended(inner, (("sy", 1), ("sx", 2)), 1)


def per_device(
    features,
    labels,
    grid,
    w_reduce,
    w_spatial,
    w_expand,
    w_class,
    dir_reduce,
    dir_spatial,
    dir_expand,
    dir_class,
    gain_mid,
    shift_mid,
    gain_out,
    shift_out,
):
    alpha_a, alpha_b = coefficients(grid)
    images, rows, cols, width = features.shape
    tiles = lax.axis_size("sy") * lax.axis_size("sx")
    count = images * rows * cols * lax.axis_size("dp") * tiles
    inner_width = w_spatial.shape[3]
    current = features
    for block in range(BLOCKS):
        flat = current.reshape(-1, width)
        first = perturbed_product(
            flat, w_reduce[block], dir_reduce[0, block], dir_reduce[1, block], alpha_a, alpha_b
        )
        first = jax.nn.relu(
            normalize(first, gain_mid[block, 0], shift_mid[block, 0], count)
        ).astype(jnp.bfloat16)
        framed = padded_tile(first.reshape(images, rows, cols, inner_width))
        patches = jnp.concatenate(
            [framed[:, i : i + rows, j : j + cols, :] for i in range(3) for j in range(3)], axis=-1
        )
        patches = patches.reshape(-1, 9 * inner_width)
        spatial_base = w_spatial[block].reshape(9 * inner_width, -1)
        spatial_a = dir_spatial[0, block].reshape(9 * inner_width, -1)
        spatial_b = dir_spatial[1, block].reshape(9 * inner_width, -1)
        second = perturbed_product(patches, spatial_base, spatial_a, spatial_b, alpha_a, alpha_b)
        second = jax.nn.relu(
            normalize(second, gain_mid[block, 1], shift_mid[block, 1], count)
        ).astype(jnp.bfloat16)
        third = perturbed_product(
            second, w_expand[block], dir_expand[0, block], dir_expand[1, block], alpha_a, alpha_b
        )
        third = normalize(third, gain_out[block], shift_out[block], count)
        current = (
            jax.nn.relu(flat.astype(jnp.float32) + third)
            .astype(jnp.bfloat16)
            .reshape(images, rows, cols, width)
        )
    pooled_part = jnp.sum(current.astype(jnp.float32), axis=(1, 2))
    pooled = (lax.psum(pooled_part, ("sy", "sx")) / (rows * cols * tiles)).astype(jnp.bfloat16)
    class_a = dir_class[0]
    class_b = dir_class[1]
    norm_base, norm_a, norm_b = lax.psum(
        (
            jnp.sum(jnp.square(w_class.astype(jnp.float32)), axis=0),
            jnp.sum(jnp.square(class_a.astype(jnp.float32)), axis=0),
            jnp.sum(jnp.square(class_b.astype(jnp.float32)), axis=0),
        ),
        "dp",
    )
    ratio_a = jnp.sqrt(norm_base) / jnp.sqrt(norm_a + EPS_NORM)
    ratio_b = jnp.sqrt(norm_base) / jnp.sqrt(norm_b + EPS_NORM)
    local_class = (
        w_class.astype(jnp.float32)
        + alpha_a * ratio_a * class_a.astype(jnp.float32)
        + alpha_b * ratio_b * class_b.astype(jnp.float32)
    ).astype(jnp.bfloat16)
    logits = jnp.dot(
        pooled,
        lax.all_gather(local_class, "dp", axis=0, tiled=True),
        preferred_element_type=jnp.float32,
    )
    summed = jnp.log(jnp.sum(jnp.exp(logits), axis=1))
    classes = lax.broadcasted_iota(jnp.int32, logits.shape, 1)
    picked = jnp.sum(jnp.where(classes == labels[:, None], logits, 0.0), axis=1)
    image_loss = summed - picked
    mean_loss = lax.psum(jnp.sum(image_loss), "dp") / (images * lax.axis_size("dp"))
    return (current, image_loss, mean_loss)


def solution(mesh):
    in_specs = (
        P("dp", "sy", "sx", None),
        P("dp"),
        P(),
        P(None, None, "dp"),
        P(None, None, None, None, "dp"),
        P(None, None, "dp"),
        P("dp", None),
        P(None, None, None, "dp"),
        P(None, None, None, None, None, "dp"),
        P(None, None, None, "dp"),
        P(None, "dp", None),
        P(),
        P(),
        P(),
        P(),
    )
    out_specs = (P("dp", "sy", "sx", None), P("dp"), P())
    return jax.shard_map(
        per_device, mesh=mesh, in_specs=in_specs, out_specs=out_specs, check_vma=False
    )
```

profile of v0, /device:TPU:0, one launch (start us, length us, event | category | flops | bytes accessed | tf_op | source)
XLA Modules:
  0.0 1203.1 jit_solution(10325314932056759414)
XLA Ops:
  4.7 1.3 multiply_multiply_fusion.5
  6.1 1.3 multiply_multiply_fusion.11
  7.4 1.3 multiply_multiply_fusion.17
  8.8 32.4 %all_gather.30 = bf16[256,64]{0,1:T(8,128)(2,1)S(1)} all-gather(bf16[256,8]{0,1:T(8,128)(2,1)S(1)} %get-tuple-element.100), channel_id=1, replica_groups=mesh['dp'=8,'sy'=2,'sx'=2] {'dp'}, dimensions={1}, use_global_device_ids=true | all-gather | bytes 36864 | tf_op jit(solution)/shard_map/all_gather | solution.py:59
  42.7 39.6 %psum.161 = f32[64]{0:T(128)S(1)} all-reduce(f32[64]{0:T(128)S(1)} %get-tuple-element.142), channel_id=1, replica_groups=mesh['dp'=8,'sy'=2,'sx'=2] {'dp','sy','sx'}, use_global_device_ids=true, to_apply=%region_4.0 | all-reduce | flops 64 | bytes 512 | tf_op jit(solution)/shard_map/psum | solution.py:64
  82.4 40.7 %psum.162 = f32[64]{0:T(128)S(1)} all-reduce(f32[64]{0:T(128)S(1)} %multiply_reduce_fusion.8), channel_id=1, replica_groups=mesh['dp'=8,'sy'=2,'sx'=2] {'dp','sy','sx'}, use_global_device_ids=true, to_apply=%region_6.0 | all-reduce | flops 64 | bytes 512 | tf_op jit(solution)/shard_map/psum | solution.py:66
  124.7 4.2 collective-permute-start
  128.8 1.3 collective-permute-start.1
  130.6 32.7 %all_gather.31 = bf16[576,64]{0,1:T(8,128)(2,1)} all-gather(bf16[576,8]{0,1:T(8,128)(2,1)S(1)} %add_convert_fusion.2), channel_id=1, replica_groups=mesh['dp'=8,'sy'=2,'sx'=2] {'dp'}, dimensions={1}, use_global_device_ids=true | all-gather | bytes 82944 | tf_op jit(solution)/shard_map/all_gather | solution.py:59
  166.4 32.6 %all_gather.34 = bf16[576,64]{0,1:T(8,128)(2,1)} all-gather(bf16[576,8]{0,1:T(8,128)(2,1)S(1)} %add_convert_fusion.1), channel_id=1, replica_groups=mesh['dp'=8,'sy'=2,'sx'=2] {'dp'}, dimensions={1}, use_global_device_ids=true | all-gather | bytes 82944 | tf_op jit(solution)/shard_map/all_gather | solution.py:59
  200.1 36.1 %all-reduce = (f32[1000]{0:T(1024)S(1)}, f32[1000]{0:T(1024)S(1)}, f32[1000]{0:T(1024)S(1)}) all-reduce(f32[1000]{0:T(1024)S(1)} %get-tuple-element.4, f32[1000]{0:T(1024)S(1)} %get-tuple-element.174, f32[1000]{0:T(1024)S(1)} %get-tuple-element.3), channel_id=1, replica_groups=mesh['dp'=8,'sy'=2,'sx'=2] {'dp'}, use_global_device_ids=true, to_apply=%region_70.71 | all-reduce | flops 3000 | bytes 24000 | tf_op jit(solution)/shard_map/psum | solution.py:130
  236.2 1.3 multiply_multiply_fusion.1
  237.6 31.2 %all_gather.39 = bf16[256,1000]{1,0:T(8,128)(2,1)S(1)} all-gather(bf16[32,1000]{1,0:T(8,128)(2,1)S(1)} %fusion.14), channel_id=1, replica_groups=mesh['dp'=8,'sy'=2,'sx'=2] {'dp'}, dimensions={0}, use_global_device_ids=true | all-gather | bytes 576000 | tf_op jit(solution)/shard_map/all_gather | solution.py:147
  268.8 1.3 multiply_multiply_fusion.15
  270.2 1.3 multiply_multiply_fusion.3
  272.2 32.5 %all_gather.32 = bf16[64,256]{0,1:T(8,128)(2,1)} all-gather(bf16[64,32]{0,1:T(8,128)(2,1)S(1)} %get-tuple-element.95), channel_id=1, replica_groups=mesh['dp'=8,'sy'=2,'sx'=2] {'dp'}, dimensions={1}, use_global_device_ids=true | all-gather | bytes 36864 | tf_op jit(solution)/shard_map/all_gather | solution.py:59
  306.2 1.3 collective-permute-start.3
  307.5 32.1 %all_gather.33 = bf16[256,64]{0,1:T(8,128)(2,1)} all-gather(bf16[256,8]{0,1:T(8,128)(2,1)S(1)} %get-tuple-element.101), channel_id=1, replica_groups=mesh['dp'=8,'sy'=2,'sx'=2] {'dp'}, dimensions={1}, use_global_device_ids=true | all-gather | bytes 36864 | tf_op jit(solution)/shard_map/all_gather | solution.py:59
  348.3 37.4 %psum.163 = f32[64]{0:T(128)S(1)} all-reduce(f32[64]{0:T(128)S(1)} %get-tuple-element.144), channel_id=1, replica_groups=mesh['dp'=8,'sy'=2,'sx'=2] {'dp','sy','sx'}, use_global_device_ids=true, to_apply=%region_11.12 | all-reduce | flops 64 | bytes 512 | tf_op jit(solution)/shard_map/psum | solution.py:64
  386.0 42.8 %psum.164 = f32[64]{0:T(128)S(1)} all-reduce(f32[64]{0:T(128)S(1)} %multiply_reduce_fusion.7), channel_id=1, replica_groups=mesh['dp'=8,'sy'=2,'sx'=2] {'dp','sy','sx'}, use_global_device_ids=true, to_apply=%region_13.14 | all-reduce | flops 64 | bytes 512 | tf_op jit(solution)/shard_map/psum | solution.py:66
  429.9 38.1 %psum.165 = f32[256]{0:T(256)S(1)} all-reduce(f32[256]{0:T(256)S(1)} %get-tuple-element.146), channel_id=1, replica_groups=mesh['dp'=8,'sy'=2,'sx'=2] {'dp','sy','sx'}, use_global_device_ids=true, to_apply=%region_18.19 | all-reduce | flops 256 | bytes 2048 | tf_op jit(solution)/shard_map/psum | solution.py:64
  468.1 41.9 %psum.166 = f32[256]{0:T(256)S(1)} all-reduce(f32[256]{0:T(256)S(1)} %multiply_reduce_fusion.2), channel_id=1, replica_groups=mesh['dp'=8,'sy'=2,'sx'=2] {'dp','sy','sx'}, use_global_device_ids=true, to_apply=%region_20.21 | all-reduce | flops 256 | bytes 2048 | tf_op jit(solution)/shard_map/psum | solution.py:66
  511.8 38.3 %psum.167 = f32[64]{0:T(128)S(1)} all-reduce(f32[64]{0:T(128)S(1)} %get-tuple-element.148), channel_id=1, replica_groups=mesh['dp'=8,'sy'=2,'sx'=2] {'dp','sy','sx'}, use_global_device_ids=true, to_apply=%region_25.26 | all-reduce | flops 64 | bytes 512 | tf_op jit(solution)/shard_map/psum | solution.py:64
  550.2 41.9 %psum.168 = f32[64]{0:T(128)S(1)} all-reduce(f32[64]{0:T(128)S(1)} %multiply_reduce_fusion.6), channel_id=1, replica_groups=mesh['dp'=8,'sy'=2,'sx'=2] {'dp','sy','sx'}, use_global_device_ids=true, to_apply=%region_27.28 | all-reduce | flops 64 | bytes 512 | tf_op jit(solution)/shard_map/psum | solution.py:66
  593.1 4.2 collective-permute-start.4
  597.3 32.5 %all_gather.35 = bf16[64,256]{0,1:T(8,128)(2,1)} all-gather(bf16[64,32]{0,1:T(8,128)(2,1)S(1)} %copy-done.24), channel_id=1, replica_groups=mesh['dp'=8,'sy'=2,'sx'=2] {'dp'}, dimensions={1}, use_global_device_ids=true | all-gather | bytes 36864 | tf_op jit(solution)/shard_map/all_gather | solution.py:59
  631.2 4.2 collective-permute-done.5
  635.6 1.3 collective-permute-start.6
  636.9 1.3 collective-permute-start.7
  638.2 30.6 %all_gather.36 = bf16[256,64]{0,1:T(8,128)(2,1)S(1)} all-gather(bf16[256,8]{0,1:T(8,128)(2,1)S(1)} %get-tuple-element.99), channel_id=1, replica_groups=mesh['dp'=8,'sy'=2,'sx'=2] {'dp'}, dimensions={1}, use_global_device_ids=true | all-gather | bytes 36864 | tf_op jit(solution)/shard_map/all_gather | solution.py:59
  672.7 1.7 copy.33
  679.1 36.9 %psum.169 = f32[64]{0:T(128)S(1)} all-reduce(f32[64]{0:T(128)S(1)} %get-tuple-element.150), channel_id=1, replica_groups=mesh['dp'=8,'sy'=2,'sx'=2] {'dp','sy','sx'}, use_global_device_ids=true, to_apply=%region_32.33 | all-reduce | flops 64 | bytes 512 | tf_op jit(solution)/shard_map/psum | solution.py:64
  716.2 41.0 %psum.170 = f32[64]{0:T(128)S(1)} all-reduce(f32[64]{0:T(128)S(1)} %multiply_reduce_fusion.5), channel_id=1, replica_groups=mesh['dp'=8,'sy'=2,'sx'=2] {'dp','sy','sx'}, use_global_device_ids=true, to_apply=%region_34.35 | all-reduce | flops 64 | bytes 512 | tf_op jit(solution)/shard_map/psum | solution.py:66
  758.3 39.7 %psum.171 = f32[256]{0:T(256)S(1)} all-reduce(f32[256]{0:T(256)S(1)} %get-tuple-element.152), channel_id=1, replica_groups=mesh['dp'=8,'sy'=2,'sx'=2] {'dp','sy','sx'}, use_global_device_ids=true, to_apply=%region_39.40 | all-reduce | flops 256 | bytes 2048 | tf_op jit(solution)/shard_map/psum | solution.py:64
  798.1 40.3 %psum.172 = f32[256]{0:T(256)S(1)} all-reduce(f32[256]{0:T(256)S(1)} %multiply_reduce_fusion.1), channel_id=1, replica_groups=mesh['dp'=8,'sy'=2,'sx'=2] {'dp','sy','sx'}, use_global_device_ids=true, to_apply=%region_41.42 | all-reduce | flops 256 | bytes 2048 | tf_op jit(solution)/shard_map/psum | solution.py:66
  839.7 39.7 %psum.173 = f32[64]{0:T(128)S(1)} all-reduce(f32[64]{0:T(128)S(1)} %get-tuple-element.154), channel_id=1, replica_groups=mesh['dp'=8,'sy'=2,'sx'=2] {'dp','sy','sx'}, use_global_device_ids=true, to_apply=%region_46.47 | all-reduce | flops 64 | bytes 512 | tf_op jit(solution)/shard_map/psum | solution.py:64
  879.5 40.3 %psum.174 = f32[64]{0:T(128)S(1)} all-reduce(f32[64]{0:T(128)S(1)} %multiply_reduce_fusion.4), channel_id=1, replica_groups=mesh['dp'=8,'sy'=2,'sx'=2] {'dp','sy','sx'}, use_global_device_ids=true, to_apply=%region_48.49 | all-reduce | flops 64 | bytes 512 | tf_op jit(solution)/shard_map/psum | solution.py:66
  920.9 4.2 collective-permute-start.8
  925.1 32.5 %all_gather.37 = bf16[576,64]{0,1:T(8,128)(2,1)} all-gather(bf16[576,8]{0,1:T(8,128)(2,1)S(1)} %add_convert_fusion), channel_id=1, replica_groups=mesh['dp'=8,'sy'=2,'sx'=2] {'dp'}, dimensions={1}, use_global_device_ids=true | all-gather | bytes 82944 | tf_op jit(solution)/shard_map/all_gather | solution.py:59
  959.0 4.2 collective-permute-done.9
  964.7 1.3 collective-permute-start.11
  966.0 32.8 %all_gather.38 = bf16[64,256]{0,1:T(8,128)(2,1)} all-gather(bf16[64,32]{0,1:T(8,128)(2,1)S(1)} %copy-done.23), channel_id=1, replica_groups=mesh['dp'=8,'sy'=2,'sx'=2] {'dp'}, dimensions={1}, use_global_device_ids=true | all-gather | bytes 36864 | tf_op jit(solution)/shard_map/all_gather | solution.py:59
  1008.1 36.9 %psum.175 = f32[64]{0:T(128)S(1)} all-reduce(f32[64]{0:T(128)S(1)} %get-tuple-element.156), channel_id=1, replica_groups=mesh['dp'=8,'sy'=2,'sx'=2] {'dp','sy','sx'}, use_global_device_ids=true, to_apply=%region_53.54 | all-reduce | flops 64 | bytes 512 | tf_op jit(solution)/shard_map/psum | solution.py:64
  1045.2 41.8 %psum.176 = f32[64]{0:T(128)S(1)} all-reduce(f32[64]{0:T(128)S(1)} %multiply_reduce_fusion.3), channel_id=1, replica_groups=mesh['dp'=8,'sy'=2,'sx'=2] {'dp','sy','sx'}, use_global_device_ids=true, to_apply=%region_55.56 | all-reduce | flops 64 | bytes 512 | tf_op jit(solution)/shard_map/psum | solution.py:66
  1088.1 38.9 %psum.177 = f32[256]{0:T(256)S(1)} all-reduce(f32[256]{0:T(256)S(1)} %get-tuple-element.158), channel_id=1, replica_groups=mesh['dp'=8,'sy'=2,'sx'=2] {'dp','sy','sx'}, use_global_device_ids=true, to_apply=%region_60.61 | all-reduce | flops 256 | bytes 2048 | tf_op jit(solution)/shard_map/psum | solution.py:64
  1127.2 41.2 %psum.178 = f32[256]{0:T(256)S(1)} all-reduce(f32[256]{0:T(256)S(1)} %multiply_reduce_fusion), channel_id=1, replica_groups=mesh['dp'=8,'sy'=2,'sx'=2] {'dp','sy','sx'}, use_global_device_ids=true, to_apply=%region_62.63 | all-reduce | flops 256 | bytes 2048 | tf_op jit(solution)/shard_map/psum | solution.py:66
  1169.3 6.0 psum.179
  1177.4 22.0 %psum.183 = f32[]{:T(128)} all-reduce(f32[]{:T(128)} %sub.104), channel_id=1, replica_groups=mesh['dp'=8,'sy'=2,'sx'=2] {'dp'}, use_global_device_ids=true, to_apply=%region_73.74 | all-reduce | flops 1 | bytes 8 | tf_op jit(solution)/shard_map/psum | solution.py:154
  (310 shorter events, 56.5 us)
Async XLA Ops:
  2.8 1.0 copy-start.17
  3.9 0.7 copy-start.22
  6.1 2.6 copy-start.20
  82.2 40.9 %copy-start.42 = (f32[3,2,64]{2,1,0:T(2,128)S(1)}, f32[3,2,64]{2,1,0:T(2,128)}, u32[]{:S(2)}) copy-start(f32[3,2,64]{2,1,0:T(2,128)} %param.26) | copy-start | bytes 4612
  82.4 40.7 %copy-start.41 = (f32[3,2,64]{2,1,0:T(2,128)S(1)}, f32[3,2,64]{2,1,0:T(2,128)}, u32[]{:S(2)}) copy-start(f32[3,2,64]{2,1,0:T(2,128)} %param.27) | copy-start | bytes 4612
  124.6 5.6 copy-start.9
  124.7 180.1 %collective-permute-start = (bf16[1,1,28,64]{3,2,1,0:T(8,128)(2,1)S(1)}, bf16[1,1,28,64]{3,2,1,0:T(8,128)(2,1)S(1)}, u32[]{:S(2)}, u32[]{:S(2)}) collective-permute-start(bf16[1,1,28,64]{3,2,1,0:T(8,128)(2,1)S(1)} %get-tuple-element.86), channel_id=1, source_target_pairs={{0,2},{1,3},{4,6},{5,7},{8,10},{9,11},{12,14},{13,15},{16,18},{17,... | collective-permute-start | bytes 10760 | tf_op jit(solution)/shard_map/ppermute | solution.py:22
  128.8 175.9 %collective-permute-start.1 = (bf16[1,1,28,64]{3,2,1,0:T(8,128)(2,1)S(1)}, bf16[1,1,28,64]{3,2,1,0:T(8,128)(2,1)S(1)}, u32[]{:S(2)}, u32[]{:S(2)}) collective-permute-start(bf16[1,1,28,64]{3,2,1,0:T(8,128)(2,1)S(1)} %get-tuple-element.85), channel_id=1, source_target_pairs={{2,0},{3,1},{6,4},{7,5},{10,8},{11,9},{14,12},{15,13},{18,16},{19,... | collective-permute-start | bytes 10760 | tf_op jit(solution)/shard_map/ppermute | solution.py:24
  130.6 32.7 %copy-start.18 = (bf16[2,3,64,32]{2,3,1,0:T(8,128)(2,1)S(1)}, bf16[2,3,64,32]{2,3,1,0:T(8,128)(2,1)}, u32[]{:S(2)}) copy-start(bf16[2,3,64,32]{2,3,1,0:T(8,128)(2,1)} %param.24) | copy-start | bytes 73732
  163.3 0.7 copy-start.21
  164.0 0.7 copy-start.43
  164.7 0.7 copy-start.44
  199.1 0.9 copy-start
  199.2 0.9 copy-start.16
  304.9 36.4 %collective-permute-start.2 = (bf16[1,30,1,64]{3,2,1,0:T(2,128)(2,1)S(1)}, bf16[1,30,1,64]{3,2,1,0:T(2,128)(2,1)S(1)}, u32[]{:S(2)}, u32[]{:S(2)}) collective-permute-start(bf16[1,30,1,64]{3,2,1,0:T(2,128)(2,1)S(1)} %get-tuple-element.71), channel_id=1, source_target_pairs={{0,1},{2,3},{4,5},{6,7},{8,9},{10,11},{12,13},{14,15},{16,17},{18,... | collective-permute-start | bytes 11528 | tf_op jit(solution)/shard_map/ppermute | solution.py:22
  306.2 35.1 %collective-permute-start.3 = (bf16[1,30,1,64]{3,2,1,0:T(2,128)(2,1)S(1)}, bf16[1,30,1,64]{3,2,1,0:T(2,128)(2,1)S(1)}, u32[]{:S(2)}, u32[]{:S(2)}) collective-permute-start(bf16[1,30,1,64]{3,2,1,0:T(2,128)(2,1)S(1)} %get-tuple-element.70), channel_id=1, source_target_pairs={{1,0},{3,2},{5,4},{7,6},{9,8},{11,10},{13,12},{15,14},{17,16},{19,... | collective-permute-start | bytes 11528 | tf_op jit(solution)/shard_map/ppermute | solution.py:24
  342.8 0.9 copy-start.3
  343.7 0.9 copy-start.6
  346.1 0.9 copy-start.1
  347.0 0.9 copy-start.11
  385.8 43.0 %copy-start.14 = (bf16[64,256]{0,1:T(8,128)(2,1)S(1)}, bf16[64,256]{0,1:T(8,128)(2,1)}, u32[]{:S(2)}) copy-start(bf16[64,256]{0,1:T(8,128)(2,1)} %all_gather.32) | copy-start | bytes 98308
  428.8 0.7 copy-start.50
  468.0 42.0 %copy-start.38 = (f32[1,256]{1,0:T(1,128)S(1)}, f32[1,256]{1,0:T(1,128)}, u32[]{:S(2)}) copy-start(f32[1,256]{1,0:T(1,128)} %get-tuple-element.108) | copy-start | bytes 3076
  510.0 0.7 copy-start.37
  510.7 0.8 copy-start.19
  593.0 4.3 copy-start.24
  593.1 38.0 %collective-permute-start.4 = (bf16[1,1,28,64]{3,2,1,0:T(8,128)(2,1)S(1)}, bf16[1,1,28,64]{3,2,1,0:T(8,128)(2,1)S(1)}, u32[]{:S(2)}, u32[]{:S(2)}) collective-permute-start(bf16[1,1,28,64]{3,2,1,0:T(8,128)(2,1)S(1)} %get-tuple-element.81), channel_id=1, source_target_pairs={{0,2},{1,3},{4,6},{5,7},{8,10},{9,11},{12,14},{13,15},{16,18},{17,... | collective-permute-start | bytes 10760 | tf_op jit(solution)/shard_map/ppermute | solution.py:22
  629.9 5.5 collective-permute-start.5
  635.6 34.3 %collective-permute-start.6 = (bf16[1,30,1,64]{3,2,1,0:T(2,128)(2,1)S(1)}, bf16[1,30,1,64]{3,2,1,0:T(2,128)(2,1)S(1)}, u32[]{:S(2)}, u32[]{:S(2)}) collective-permute-start(bf16[1,30,1,64]{3,2,1,0:T(2,128)(2,1)S(1)} %get-tuple-element.66), channel_id=1, source_target_pairs={{0,1},{2,3},{4,5},{6,7},{8,9},{10,11},{12,13},{14,15},{16,17},{18,... | collective-permute-start | bytes 11528 | tf_op jit(solution)/shard_map/ppermute | solution.py:22
  636.9 33.0 %collective-permute-start.7 = (bf16[1,30,1,64]{3,2,1,0:T(2,128)(2,1)S(1)}, bf16[1,30,1,64]{3,2,1,0:T(2,128)(2,1)S(1)}, u32[]{:S(2)}, u32[]{:S(2)}) collective-permute-start(bf16[1,30,1,64]{3,2,1,0:T(2,128)(2,1)S(1)} %get-tuple-element.65), channel_id=1, source_target_pairs={{1,0},{3,2},{5,4},{7,6},{9,8},{11,10},{13,12},{15,14},{17,16},{19,... | collective-permute-start | bytes 11528 | tf_op jit(solution)/shard_map/ppermute | solution.py:24
  674.5 0.9 copy-start.4
  675.4 0.9 copy-start.7
  677.8 0.9 copy-start.10
  716.0 41.2 %copy-start.13 = (bf16[64,256]{0,1:T(8,128)(2,1)S(1)}, bf16[64,256]{0,1:T(8,128)(2,1)}, u32[]{:S(2)}) copy-start(bf16[64,256]{0,1:T(8,128)(2,1)} %all_gather.35) | copy-start | bytes 98308
  798.0 40.4 %copy-start.36 = (f32[1,256]{1,0:T(1,128)S(1)}, f32[1,256]{1,0:T(1,128)}, u32[]{:S(2)}) copy-start(f32[1,256]{1,0:T(1,128)} %get-tuple-element.107) | copy-start | bytes 3076
  838.4 0.7 copy-start.35
  920.9 38.0 %collective-permute-start.8 = (bf16[1,1,28,64]{3,2,1,0:T(8,128)(2,1)S(1)}, bf16[1,1,28,64]{3,2,1,0:T(8,128)(2,1)S(1)}, u32[]{:S(2)}, u32[]{:S(2)}) collective-permute-start(bf16[1,1,28,64]{3,2,1,0:T(8,128)(2,1)S(1)} %get-tuple-element.76), channel_id=1, source_target_pairs={{0,2},{1,3},{4,6},{5,7},{8,10},{9,11},{12,14},{13,15},{16,18},{17,... | collective-permute-start | bytes 10760 | tf_op jit(solution)/shard_map/ppermute | solution.py:22
  957.6 5.5 collective-permute-start.9
  963.3 2.6 copy-start.23
  963.4 37.7 %collective-permute-start.10 = (bf16[1,30,1,64]{3,2,1,0:T(2,128)(2,1)S(1)}, bf16[1,30,1,64]{3,2,1,0:T(2,128)(2,1)S(1)}, u32[]{:S(2)}, u32[]{:S(2)}) collective-permute-start(bf16[1,30,1,64]{3,2,1,0:T(2,128)(2,1)S(1)} %get-tuple-element.61), channel_id=1, source_target_pairs={{0,1},{2,3},{4,5},{6,7},{8,9},{10,11},{12,13},{14,15},{16,17},{18,... | collective-permute-start | bytes 11528 | tf_op jit(solution)/shard_map/ppermute | solution.py:22
  964.7 36.4 %collective-permute-start.11 = (bf16[1,30,1,64]{3,2,1,0:T(2,128)(2,1)S(1)}, bf16[1,30,1,64]{3,2,1,0:T(2,128)(2,1)S(1)}, u32[]{:S(2)}, u32[]{:S(2)}) collective-permute-start(bf16[1,30,1,64]{3,2,1,0:T(2,128)(2,1)S(1)} %get-tuple-element.60), channel_id=1, source_target_pairs={{1,0},{3,2},{5,4},{7,6},{9,8},{11,10},{13,12},{15,14},{17,16},{19,... | collective-permute-start | bytes 11528 | tf_op jit(solution)/shard_map/ppermute | solution.py:24
  1002.6 0.9 copy-start.5
  1003.5 0.9 copy-start.8
  1005.9 0.9 copy-start.2
  1006.8 0.9 copy-start.12
  1045.0 42.0 %copy-start.15 = (bf16[64,256]{0,1:T(8,128)(2,1)S(1)}, bf16[64,256]{0,1:T(8,128)(2,1)}, u32[]{:S(2)}) copy-start(bf16[64,256]{0,1:T(8,128)(2,1)} %all_gather.38) | copy-start | bytes 98308
  1127.0 41.3 %copy-start.40 = (f32[1,256]{1,0:T(1,128)S(1)}, f32[1,256]{1,0:T(1,128)}, u32[]{:S(2)}) copy-start(f32[1,256]{1,0:T(1,128)} %get-tuple-element.109) | copy-start | bytes 3076
  1168.3 0.7 copy-start.39
  (21 other events, 13.0 us)
where the time goes:
time: 1210 us; the launch traced here: 1200 us
  blocking collectives  1100 us (91%)
  local copies, waits for them, and re-layouts  39.7 us (3%)
  starting transfers between devices  24.1 us (2%)
  other arithmetic  17.3 us (1%)
    psum x9, blocking collectives, normalize(): lax.psum(jnp.sum(centred * centred, axis=0), ('dp', 'sy', 'sx')) / count  372 us
    psum x9, blocking collectives, normalize(): mean = lax.psum(jnp.sum(y, axis=0), ('dp', 'sy', 'sx')) / count  345 us
    all_gather x9, blocking collectives, perturbed_product(): lax.all_gather(local, 'dp', axis=1, tiled=True)  291 us
    psum x1, blocking collectives, per_device(): lax.psum((jnp.sum(jnp.square(w_class.astype(jnp.float32)), axis=0), jnp.s...  36.1 us
    all_gather x1, blocking collectives, per_device(): lax.all_gather(local_class, 'dp', axis=0, tiled=True)  31.2 us
  transfers between devices with their start and end apart: 12, of which 2 were waited for; matrix products, arithmetic and copies ran while one was open for 1% of the time, Pallas kernels for 0%

commit v1 on v0

--- a/solution.py
+++ b/solution.py
@@ -1,6 +1,10 @@
+import functools
+
 import jax
 import jax.numpy as jnp
 from jax import lax
+from jax.experimental import pallas as pl
+from jax.experimental.pallas import tpu as pltpu
 from jax.sharding import PartitionSpec as P
 
 BLOCKS = 3
@@ -155,6 +159,393 @@
     return (current, image_loss, mean_loss)
 
 
+F32 = jnp.float32
+BF16 = jnp.bfloat16
+NT = (((1,), (1,)), ((), ()))
+
+
+def round_up(value, unit):
+    return (value + unit - 1) // unit * unit
+
+
+def rows_joined(blocks):
+    count, rows, width = blocks.shape
+    if rows % 16 == 0:
+        return blocks.reshape(count * rows, width)
+    return blocks.astype(F32).reshape(count * rows, width).astype(BF16)
+
+
+def unit_ratio(base_sq, dir_sq):
+    return jnp.sqrt(base_sq) / jnp.sqrt(dir_sq + EPS_NORM)
+
+
+def section_kernel(
+    parts,
+    x_ref,
+    labels_ref,
+    grid_ref,
+    wr_ref,
+    ws_ref,
+    we_ref,
+    wc_ref,
+    dr_ref,
+    ds_ref,
+    de_ref,
+    dc_ref,
+    gm_ref,
+    sm_ref,
+    go_ref,
+    so_ref,
+    out_ref,
+    loss_ref,
+    mean_ref,
+    xs,
+    edge,
+    y2s,
+    y3s,
+    pr,
+    ps,
+    pe,
+    pc,
+    nc,
+    tile_mid,
+    tile_out,
+    all_mid,
+    all_out,
+    halo_row,
+    halo_col,
+    halo_cor,
+    pooled_parts,
+    loss_parts,
+    send,
+    recv,
+):
+    rows, cols, width = x_ref.shape
+    blocks = wr_ref.shape[0]
+    mid = edge.shape[-1]
+    pitch = edge.shape[1]
+    flat = rows * pitch
+    classes = wc_ref.shape[-1]
+    last = pitch - 8
+    me, my_y, my_x = lax.axis_index("dp"), lax.axis_index("sy"), lax.axis_index("sx")
+    tile = my_y * 2 + my_x
+    across = {"sy": 1 - my_y}
+    beside = {"sx": 1 - my_x}
+    corner = {"sy": 1 - my_y, "sx": 1 - my_x}
+    quad = (beside, across, corner)
+
+    def peer(d):
+        return {"dp": lax.rem(me + d, parts)}
+
+    def each_part(act):
+        def step(d, carry):
+            act(peer(d))
+            return carry
+
+        lax.fori_loop(1, parts, step, 0)
+
+    counter = [0]
+
+    def channel():
+        counter[0] += 1
+        return counter[0] - 1
+
+    def push(source, target, link, device):
+        pltpu.make_async_remote_copy(
+            src_ref=source,
+            dst_ref=target,
+            send_sem=send.at[link],
+            recv_sem=recv.at[link],
+            device_id=device,
+            device_id_type=pl.DeviceIdType.MESH,
+        ).start()
+
+    def arrived(view, link):
+        pltpu.make_async_copy(view, view, recv.at[link]).wait()
+
+    def left(view, link):
+        pltpu.make_async_copy(view, view, send.at[link]).wait()
+
+    pending = []
+
+    def share_parts(buffer):
+        link = channel()
+        own = buffer.at[me]
+        each_part(lambda device: push(own, own, link, device))
+        view = buffer.at[pl.ds(0, parts - 1)]
+        pending.append((view, link))
+        return lambda: arrived(view, link)
+
+    def share_tiles(buffer):
+        link = channel()
+        own = buffer.at[tile]
+        for device in quad:
+            push(own, own, link, device)
+        view = buffer.at[pl.ds(0, 3)]
+        pending.append((view, link))
+        return lambda: arrived(view, link)
+
+    barrier = pltpu.get_barrier_semaphore()
+
+    def greet(device):
+        pl.semaphore_signal(barrier, inc=1, device_id=device, device_id_type=pl.DeviceIdType.MESH)
+
+    for device in quad:
+        greet(device)
+    each_part(greet)
+
+    alpha = [(2.0 * grid_ref[k].astype(F32) + (1.0 - GRID)) * (1.0 / GRID) for k in range(2)]
+
+    def square_sum(value):
+        return jnp.sum(value * value, axis=-1, keepdims=True)
+
+    for b in range(blocks):
+        base, first, second = (v.astype(F32) for v in (wr_ref[b], dr_ref[0, b], dr_ref[1, b]))
+        norm = square_sum(base)
+        pr[me, b] = (
+            base
+            + alpha[0] * unit_ratio(norm, square_sum(first)) * first
+            + alpha[1] * unit_ratio(norm, square_sum(second)) * second
+        ).astype(BF16)
+    pl.semaphore_wait(barrier, 3 + parts - 1)
+    have_reduce = share_parts(pr)
+    for b in range(blocks):
+        base, first, second = (v.astype(F32) for v in (ws_ref[b], ds_ref[0, b], ds_ref[1, b]))
+        norm, norm_a, norm_b = (
+            jnp.sum(square_sum(v), axis=0) for v in (base, first, second)
+        )
+        value = (
+            base
+            + (alpha[0] * unit_ratio(norm, norm_a))[None] * first
+            + (alpha[1] * unit_ratio(norm, norm_b))[None] * second
+        )
+        ps[me, b] = jnp.concatenate([value[t] for t in range(value.shape[0])], axis=-1).astype(BF16)
+    have_spatial = share_parts(ps)
+    for b in range(blocks):
+        base, first, second = (v.astype(F32) for v in (we_ref[b], de_ref[0, b], de_ref[1, b]))
+        norm = square_sum(base)
+        pe[me, b] = (
+            base
+            + alpha[0] * unit_ratio(norm, square_sum(first)) * first
+            + alpha[1] * unit_ratio(norm, square_sum(second)) * second
+        ).astype(BF16)
+    have_expand = share_parts(pe)
+    class_arrays = [v.astype(F32) for v in (wc_ref[...], dc_ref[0], dc_ref[1])]
+    nc[me] = jnp.concatenate(
+        [jnp.sum(v * v, axis=0, keepdims=True) for v in class_arrays], axis=0
+    )
+    have_norms = share_parts(nc)
+
+    xs[...] = jnp.zeros_like(xs)
+    xs[:, 0:cols, :] = x_ref[...]
+
+    inside = lax.broadcasted_iota(jnp.int32, (rows, pitch, 1), 1) < cols
+    edge_row = lax.broadcasted_iota(jnp.int32, (rows + 2, pitch, 1), 0)
+    edge_col = lax.broadcasted_iota(jnp.int32, (rows + 2, pitch, 1), 1)
+    far_row = jnp.where(my_y == 0, rows + 1, 0)
+    far_col = jnp.where(my_x == 0, cols, pitch - 1)
+    valid = ((edge_row >= 1) & (edge_row <= rows) | (edge_row == far_row)) & (
+        (edge_col < cols) | (edge_col == far_col)
+    )
+    near_row = jnp.where(my_y == 0, rows, 1)
+    near_col = pl.multiple_of(jnp.where(my_x == 0, last, 0), 8)
+    slot = far_col - last
+
+    def local_stats(value):
+        masked = jnp.where(inside, value, 0.0)
+        mean = jnp.sum(masked, axis=(0, 1), keepdims=True)[0] / (rows * cols)
+        centred = jnp.where(inside, value - mean[None], 0.0)
+        return mean, jnp.sum(centred * centred, axis=(0, 1), keepdims=True)[0] / (rows * cols)
+
+    def pooled_stats(buffer, r):
+        means, spreads = buffer[r, :, 0:1, :], buffer[r, :, 1:2, :]
+        mean = jnp.mean(means, axis=0)
+        gap = means - mean[None]
+        return mean, jnp.mean(spreads, axis=0) + jnp.mean(gap * gap, axis=0)
+
+    def batch_stats(value, tiles, alls, r):
+        mean, var = local_stats(value)
+        tiles[r, tile, 0:1, :] = mean
+        tiles[r, tile, 1:2, :] = var
+        share_tiles(tiles.at[r])()
+        mean, var = pooled_stats(tiles, r)
+        alls[r, me, 0:1, :] = mean
+        alls[r, me, 1:2, :] = var
+        share_parts(alls.at[r])()
+        mean, var = pooled_stats(alls, r)
+        return mean, lax.rsqrt(var + EPS_BN)
+
+    for b in range(blocks):
+        if b == 0:
+            have_reduce()
+        w = rows_joined(pr[:, b])
+        y = lax.dot_general(xs[...].reshape(flat, width), w, NT, preferred_element_type=F32)
+        edge[1 : rows + 1] = y.reshape(rows, pitch, mid)
+        links = (channel(), channel(), channel())
+        push(edge.at[near_row], halo_row.at[b], links[0], across)
+        push(
+            edge.at[pl.ds(1, rows), pl.ds(near_col, 8), :], halo_col.at[b], links[1], beside
+        )
+        push(edge.at[near_row, pl.ds(near_col, 8), :], halo_cor.at[b], links[2], corner)
+        mean, scale = batch_stats(edge[1 : rows + 1], tile_mid, all_mid, 2 * b)
+        for view, link in zip((halo_row.at[b], halo_col.at[b], halo_cor.at[b]), links):
+            left(view, link)
+            arrived(view, link)
+        shifted = pltpu.roll(halo_col[b].reshape(rows * 8, mid), 4, 0).reshape(rows, 8, mid)
+        lane8 = lax.broadcasted_iota(jnp.int32, (rows, 8, 1), 1)
+        edge[1 : rows + 1, last:pitch, :] = jnp.where(
+            lane8 == slot, shifted, edge[1 : rows + 1, last:pitch, :]
+        )
+        edge[far_row] = halo_row[b]
+        end8 = lax.broadcasted_iota(jnp.int32, (8, 1), 0)
+        edge[far_row, last:pitch, :] = jnp.where(
+            end8 == slot, pltpu.roll(halo_cor[b], 4, 0), halo_row[b, last:pitch, :]
+        )
+        gain = scale * gm_ref[b, 0:1]
+        a = jnp.where(
+            valid,
+            jax.nn.relu((edge[...] - mean[None]) * gain[None] + sm_ref[b, 0:1][None]),
+            0.0,
+        )
+        tall = (rows + 2) * pitch
+        prev = pltpu.roll(a, 1, 1).reshape(tall, mid)
+        after = pltpu.roll(a, pitch - 1, 1).reshape(tall, mid)
+        wide = jnp.concatenate([prev, a.reshape(tall, mid), after], axis=-1).astype(BF16)
+        if b == 0:
+            have_norms()
+            sums = jnp.sum(nc[...], axis=0)
+            base_sq = sums[0:1]
+            pc[me] = (
+                class_arrays[0]
+                + alpha[0] * unit_ratio(base_sq, sums[1:2]) * class_arrays[1]
+                + alpha[1] * unit_ratio(base_sq, sums[2:3]) * class_arrays[2]
+            ).astype(BF16)
+            have_class = share_parts(pc)
+            have_spatial()
+        w = rows_joined(ps[:, b])
+        span = 3 * mid
+        y = sum(
+            lax.dot_general(
+                wide[i * pitch : i * pitch + flat],
+                w[:, i * span : (i + 1) * span],
+                NT,
+                preferred_element_type=F32,
+            )
+            for i in range(3)
+        )
+        y2s[...] = y.reshape(rows, pitch, mid)
+        mean, scale = batch_stats(y2s[...], tile_mid, all_mid, 2 * b + 1)
+        gain = scale * gm_ref[b, 1:2]
+        c = jax.nn.relu((y2s[...] - mean[None]) * gain[None] + sm_ref[b, 1:2][None])
+        if b == 0:
+            have_expand()
+        w = rows_joined(pe[:, b])
+        y = lax.dot_general(
+            c.reshape(flat, mid).astype(BF16), w, NT, preferred_element_type=F32
+        )
+        y3s[...] = y.reshape(rows, pitch, width)
+        mean, scale = batch_stats(y3s[...], tile_out, all_out, b)
+        gain = scale * go_ref[b : b + 1]
+        e = (y3s[...] - mean[None]) * gain[None] + so_ref[b : b + 1][None]
+        xs[...] = jnp.where(inside, jax.nn.relu(xs[...].astype(F32) + e), 0.0).astype(BF16)
+
+    final = xs[...]
+    pooled_parts[tile] = jnp.sum(final.astype(F32), axis=(0, 1), keepdims=True)[0]
+    have_pooled = share_tiles(pooled_parts)
+    out_ref[...] = xs[:, 0:cols, :]
+    have_class()
+    have_pooled()
+    total = jnp.sum(pooled_parts[...], axis=0)
+    pooled = (total / (rows * cols * 4)).astype(BF16)
+    logits = jnp.dot(pooled, rows_joined(pc[...]), preferred_element_type=F32)
+    summed = jnp.log(jnp.sum(jnp.exp(logits), axis=1, keepdims=True))
+    index = lax.broadcasted_iota(jnp.int32, logits.shape, 1)
+    picked = jnp.sum(jnp.where(index == labels_ref[0], logits, 0.0), axis=1, keepdims=True)
+    loss = jnp.broadcast_to(summed - picked, loss_ref.shape)
+    loss_ref[...] = loss
+    loss_parts[me] = loss
+    share_parts(loss_parts)()
+    mean_ref[...] = jnp.mean(loss_parts[...], axis=0)
+    for view, link in pending:
+        left(view, link)
+
+
+def fused(mesh, *args):
+    (features, labels, grid, w_reduce, w_spatial, w_expand, w_class) = args[:7]
+    (dir_reduce, dir_spatial, dir_expand, dir_class) = args[7:11]
+    parts = mesh.shape["dp"]
+    _, rows, cols, width = features.shape
+    blocks, mid = w_expand.shape[0], w_expand.shape[1]
+    taps = w_spatial.shape[1] * w_spatial.shape[2]
+    own_mid, own_out = w_reduce.shape[-1], w_expand.shape[-1]
+    own_feat, classes = w_class.shape
+    pitch = round_up(cols + 2, 8)
+
+    def spatial(v, lead):
+        return jnp.swapaxes(v, -1, -2).reshape(lead + (taps, own_mid, mid))
+
+    operands = (
+        features[0],
+        labels,
+        grid,
+        jnp.swapaxes(w_reduce, -1, -2),
+        spatial(w_spatial, (blocks,)),
+        jnp.swapaxes(w_expand, -1, -2),
+        w_class,
+        jnp.swapaxes(dir_reduce, -1, -2),
+        spatial(dir_spatial, (2, blocks)),
+        jnp.swapaxes(dir_expand, -1, -2),
+        dir_class,
+    ) + tuple(args[11:])
+    vmem = pl.BlockSpec(memory_space=pltpu.VMEM)
+    smem = pl.BlockSpec(memory_space=pltpu.SMEM)
+    links = 7 + 9 * blocks
+    out, loss, mean_loss = pl.pallas_call(
+        functools.partial(section_kernel, parts),
+        out_shape=(
+            jax.ShapeDtypeStruct((rows, cols, width), BF16),
+            jax.ShapeDtypeStruct((1, 128), F32),
+            jax.ShapeDtypeStruct((1, 128), F32),
+        ),
+        in_specs=[vmem, smem, smem] + [vmem] * 12,
+        out_specs=(vmem, vmem, vmem),
+        scratch_shapes=[
+            pltpu.VMEM((rows, pitch, width), BF16),
+            pltpu.VMEM((rows + 2, pitch, mid), F32),
+            pltpu.VMEM((rows, pitch, mid), F32),
+            pltpu.VMEM((rows, pitch, width), F32),
+            pltpu.VMEM((parts, blocks, own_mid, width), BF16),
+            pltpu.VMEM((parts, blocks, own_mid, taps * mid), BF16),
+            pltpu.VMEM((parts, blocks, own_out, mid), BF16),
+            pltpu.VMEM((parts, own_feat, classes), BF16),
+            pltpu.VMEM((parts, 3, classes), F32),
+            pltpu.VMEM((2 * blocks, 4, 2, mid), F32),
+            pltpu.VMEM((blocks, 4, 2, width), F32),
+            pltpu.VMEM((2 * blocks, parts, 2, mid), F32),
+            pltpu.VMEM((blocks, parts, 2, width), F32),
+            pltpu.VMEM((blocks, pitch, mid), F32),
+            pltpu.VMEM((blocks, rows, 8, mid), F32),
+            pltpu.VMEM((blocks, 8, mid), F32),
+            pltpu.VMEM((4, 1, width), F32),
+            pltpu.VMEM((parts, 1, 128), F32),
+            pltpu.SemaphoreType.DMA((links,)),
+            pltpu.SemaphoreType.DMA((links,)),
+        ],
+        compiler_params=pltpu.CompilerParams(
+            collective_id=0, has_side_effects=True, vmem_limit_bytes=56 * 2**20
+        ),
+    )(*operands)
+    return out[None], loss[0, 0:1], mean_loss[0, 0]
+
+
+def body(mesh, *args):
+    features = args[0]
+    plain = mesh.shape["sy"] == 2 and mesh.shape["sx"] == 2 and mesh.shape["dp"] > 1
+    if plain and features.shape[0] == 1 and features.shape[2] % 8 == 4:
+        return fused(mesh, *args)
+    return per_device(*args)
+
+
 def solution(mesh):
     in_specs = (
         P("dp", "sy", "sx", None),
@@ -175,5 +566,5 @@
     )
     out_specs = (P("dp", "sy", "sx", None), P("dp"), P())
     return jax.shard_map(
-        per_device, mesh=mesh, in_specs=in_specs, out_specs=out_specs, check_vma=False
-    )
+        functools.partial(body, mesh), mesh=mesh, in_specs=in_specs, out_specs=out_specs, check_vma=False
+    )

time: 1210 us -> 103 us (0.09)
  blocking collectives: 1100 us -> 0 us
  Pallas kernels: 0 us -> 96.7 us
  local copies, waits for them, and re-layouts: 39.7 us -> 2.46 us
  starting transfers between devices: 24.1 us -> 0 us
  other arithmetic: 17.3 us -> 0 us
    psum x21 -> x0, blocking collectives: 781 us -> none  [the longest x9 372 us: normalize(): lax.psum(jnp.sum(centred * centred, axis=0), ('dp', 'sy', 'sx')) / count]
    all_gather x10 -> x0, blocking collectives: 322 us -> none  [the longest x9 291 us: perturbed_product(): lax.all_gather(local, 'dp', axis=1, tiled=True)]
    pallas_call x0 -> x1, Pallas kernels: none -> 96.7 us  [fused(): pl.pallas_call(functools.partial(section_kernel, parts), out_shape=(jax.S...]
    ppermute x12 -> x0, starting transfers between devices: 24.1 us -> none  [the longest x6 16.4 us: extended(): lax.ppermute(tail, axis, [(i, (i + 1) % count) for i in range(ends)])]
    unnamed x138 -> x5, local copies, waits for them, and re-layouts: 21.2 us -> 2.46 us
    concatenate x54 -> x0, local copies, waits for them, and re-layouts: 12.5 us -> none  [the longest x51 12.5 us: per_device(): jnp.concatenate([framed[:, i:i + rows, j:j + cols, :] for i in range(3) f...]
  transfers between devices with their start and end apart: 12 -> 0, of which waited for: 2 -> 0; matrix products, arithmetic and copies ran while one was open for 1% -> 0% of each run, Pallas kernels for 0% -> 0%
where the time goes in v1:
time: 103 us
  Pallas kernels  96.7 us (94%)
  between operations  3.63 us (4%)
  local copies, waits for them, and re-layouts  2.46 us (2%)
    pallas_call x1, Pallas kernels, fused(): pl.pallas_call(functools.partial(section_kernel, parts), out_shape=(jax.S...  96.7 us
    unnamed x5, local copies, waits for them, and re-layouts  2.46 us

profile of v1, /device:TPU:0, one launch (start us, length us, event | category | flops | bytes accessed | tf_op | source)
XLA Modules:
  0.0 102.8 jit_solution(1593415445893125822)
XLA Ops:
  1.3 96.7 %shard_map.166 = (bf16[28,28,256]{2,1,0:T(8,128)(2,1)}, f32[1,128]{1,0:T(1,128)}, f32[1,128]{1,0:T(1,128)}) custom-call(bf16[28,28,256]{2,1,0:T(8,128)(2,1)} %bitcast.16, s32[1]{0:T(128)S(6)} %copy.21.labels_ref, s32[2]{0:T(128)} %grid_ref.1, bf16[3,8,256]{2,1,0:T(8,128)(2,1)} %bitcast.23, bf16[3,9,8,64]{3,2,1,0:T(8,128)(2,1)} %bitcast.19, ...), custom_call_target="tpu_custom_call" | custom-call | tf_op jit(solution)/shard_map/pallas_call | solution.py:503
  98.0 0.0 copy-start.1
  98.0 1.8 %copy.22 = bf16[1,28,28,256]{3,2,1,0:T(8,128)(2,1)} copy(bf16[1,28,28,256]{3,2,1,0:T(8,128)(2,1)} %bitcast.17) | data formatting | bytes 802816
  99.8 0.0 copy-done.1
  99.8 0.0 copy-start
  99.9 0.6 copy-done
Async XLA Ops:
  98.0 1.8 %copy-start.1 = (f32[1,128]{1,0:T(1,128)S(1)}, f32[1,128]{1,0:T(1,128)}, u32[]{:S(2)}) copy-start(f32[1,128]{1,0:T(1,128)} %get-tuple-element.7) | copy-start | bytes 1540
  99.8 0.7 copy-start

commit v2 on v1

--- a/solution.py
+++ b/solution.py
@@ -208,15 +208,12 @@
     pe,
     pc,
     nc,
-    tile_mid,
-    tile_out,
     all_mid,
     all_out,
     halo_row,
     halo_col,
     halo_cor,
     pooled_parts,
-    loss_parts,
     send,
     recv,
 ):
@@ -228,11 +225,12 @@
     classes = wc_ref.shape[-1]
     last = pitch - 8
     me, my_y, my_x = lax.axis_index("dp"), lax.axis_index("sy"), lax.axis_index("sx")
-    tile = my_y * 2 + my_x
+    tiles = 4
+    devices = parts * tiles
+    place = (me * 2 + my_y) * 2 + my_x
     across = {"sy": 1 - my_y}
     beside = {"sx": 1 - my_x}
     corner = {"sy": 1 - my_y, "sx": 1 - my_x}
-    quad = (beside, across, corner)
 
     def peer(d):
         return {"dp": lax.rem(me + d, parts)}
@@ -276,12 +274,22 @@
         pending.append((view, link))
         return lambda: arrived(view, link)
 
-    def share_tiles(buffer):
+    def share_all(buffer):
         link = channel()
-        own = buffer.at[tile]
-        for device in quad:
+        own = buffer.at[place]
+
+        def step(d, carry):
+            other = lax.rem(place + d, devices)
+            device = {
+                "dp": lax.div(other, tiles),
+                "sy": lax.rem(lax.div(other, 2), 2),
+                "sx": lax.rem(other, 2),
+            }
             push(own, own, link, device)
-        view = buffer.at[pl.ds(0, 3)]
+            return carry
+
+        lax.fori_loop(1, devices, step, 0)
+        view = buffer.at[pl.ds(0, devices - 1)]
         pending.append((view, link))
         return lambda: arrived(view, link)
 
@@ -290,26 +298,37 @@
     def greet(device):
         pl.semaphore_signal(barrier, inc=1, device_id=device, device_id_type=pl.DeviceIdType.MESH)
 
-    for device in quad:
-        greet(device)
-    each_part(greet)
+    def greet_step(d, carry):
+        other = lax.rem(place + d, devices)
+        greet(
+            {
+                "dp": lax.div(other, tiles),
+                "sy": lax.rem(lax.div(other, 2), 2),
+                "sx": lax.rem(other, 2),
+            }
+        )
+        return carry
+
+    lax.fori_loop(1, devices, greet_step, 0)
 
     alpha = [(2.0 * grid_ref[k].astype(F32) + (1.0 - GRID)) * (1.0 / GRID) for k in range(2)]
 
     def square_sum(value):
         return jnp.sum(value * value, axis=-1, keepdims=True)
 
-    for b in range(blocks):
-        base, first, second = (v.astype(F32) for v in (wr_ref[b], dr_ref[0, b], dr_ref[1, b]))
+    def pointwise_filters(base_ref, dir_ref, target, b):
+        base, first, second = (v.astype(F32) for v in (base_ref[b], dir_ref[0, b], dir_ref[1, b]))
         norm = square_sum(base)
-        pr[me, b] = (
+        target[b, me] = (
             base
             + alpha[0] * unit_ratio(norm, square_sum(first)) * first
             + alpha[1] * unit_ratio(norm, square_sum(second)) * second
         ).astype(BF16)
-    pl.semaphore_wait(barrier, 3 + parts - 1)
-    have_reduce = share_parts(pr)
-    for b in range(blocks):
+
+    def send_reduce(b):
+        have[("r", b)] = share_parts(pr.at[b])
+
+    def send_spatial(b):
         base, first, second = (v.astype(F32) for v in (ws_ref[b], ds_ref[0, b], ds_ref[1, b]))
         norm, norm_a, norm_b = (
             jnp.sum(square_sum(v), axis=0) for v in (base, first, second)
@@ -319,22 +338,44 @@
             + (alpha[0] * unit_ratio(norm, norm_a))[None] * first
             + (alpha[1] * unit_ratio(norm, norm_b))[None] * second
         )
-        ps[me, b] = jnp.concatenate([value[t] for t in range(value.shape[0])], axis=-1).astype(BF16)
-    have_spatial = share_parts(ps)
-    for b in range(blocks):
-        base, first, second = (v.astype(F32) for v in (we_ref[b], de_ref[0, b], de_ref[1, b]))
-        norm = square_sum(base)
-        pe[me, b] = (
+        ps[b, me] = jnp.concatenate([value[t] for t in range(value.shape[0])], axis=-1).astype(BF16)
+        have[("s", b)] = share_parts(ps.at[b])
+
+    def send_expand(b):
+        pointwise_filters(we_ref, de_ref, pe, b)
+        have[("e", b)] = share_parts(pe.at[b])
+
+    def class_arrays():
+        return [v.astype(F32) for v in (wc_ref[...], dc_ref[0], dc_ref[1])]
+
+    def send_norms():
+        nc[me] = jnp.concatenate(
+            [jnp.sum(v * v, axis=0, keepdims=True) for v in class_arrays()], axis=0
+        )
+        have["norms"] = share_parts(nc)
+
+    def send_class():
+        have["norms"]()
+        sums = jnp.sum(nc[...], axis=0)
+        base_sq = sums[0:1]
+        base, first, second = class_arrays()
+        pc[me] = (
             base
-            + alpha[0] * unit_ratio(norm, square_sum(first)) * first
-            + alpha[1] * unit_ratio(norm, square_sum(second)) * second
+            + alpha[0] * unit_ratio(base_sq, sums[1:2]) * first
+            + alpha[1] * unit_ratio(base_sq, sums[2:3]) * second
         ).astype(BF16)
-    have_expand = share_parts(pe)
-    class_arrays = [v.astype(F32) for v in (wc_ref[...], dc_ref[0], dc_ref[1])]
-    nc[me] = jnp.concatenate(
-        [jnp.sum(v * v, axis=0, keepdims=True) for v in class_arrays], axis=0
-    )
-    have_norms = share_parts(nc)
+        have["class"] = share_parts(pc)
+
+    def ready(kind, source, b):
+        have[(kind, b)]()
+        return rows_joined(source[b])
+
+    have = {}
+    pointwise_filters(wr_ref, dr_ref, pr, 0)
+    pl.semaphore_wait(barrier, devices - 1)
+    send_reduce(0)
+    send_spatial(0)
+    send_expand(0)
 
     xs[...] = jnp.zeros_like(xs)
     xs[:, 0:cols, :] = x_ref[...]
@@ -363,23 +404,43 @@
         gap = means - mean[None]
         return mean, jnp.mean(spreads, axis=0) + jnp.mean(gap * gap, axis=0)
 
-    def batch_stats(value, tiles, alls, r):
+    def batch_stats(value, alls, r, meanwhile):
         mean, var = local_stats(value)
-        tiles[r, tile, 0:1, :] = mean
-        tiles[r, tile, 1:2, :] = var
-        share_tiles(tiles.at[r])()
-        mean, var = pooled_stats(tiles, r)
-        alls[r, me, 0:1, :] = mean
-        alls[r, me, 1:2, :] = var
-        share_parts(alls.at[r])()
+        alls[r, place, 0:1, :] = mean
+        alls[r, place, 1:2, :] = var
+        come = share_all(alls.at[r])
+        other = meanwhile()
+        come()
         mean, var = pooled_stats(alls, r)
-        return mean, lax.rsqrt(var + EPS_BN)
-
+        return mean, lax.rsqrt(var + EPS_BN), other
+
+    def after_first(b):
+        if b == 0:
+            send_norms()
+        elif b == 1 and blocks > 1:
+            send_class()
+        return ready("s", ps, b)
+
+    def after_second(b):
+        if b + 1 < blocks:
+            pointwise_filters(wr_ref, dr_ref, pr, b + 1)
+            send_reduce(b + 1)
+            send_spatial(b + 1)
+        return ready("e", pe, b)
+
+    def after_third(b):
+        if b + 1 < blocks:
+            send_expand(b + 1)
+            return ready("r", pr, b + 1)
+        if "class" not in have:
+            send_class()
+        return None
+
+    w_reduce = ready("r", pr, 0)
     for b in range(blocks):
-        if b == 0:
-            have_reduce()
-        w = rows_joined(pr[:, b])
-        y = lax.dot_general(xs[...].reshape(flat, width), w, NT, preferred_element_type=F32)
+        y = lax.dot_general(
+            xs[...].reshape(flat, width), w_reduce, NT, preferred_element_type=F32
+        )
         edge[1 : rows + 1] = y.reshape(rows, pitch, mid)
         links = (channel(), channel(), channel())
         push(edge.at[near_row], halo_row.at[b], links[0], across)
@@ -387,7 +448,9 @@
             edge.at[pl.ds(1, rows), pl.ds(near_col, 8), :], halo_col.at[b], links[1], beside
         )
         push(edge.at[near_row, pl.ds(near_col, 8), :], halo_cor.at[b], links[2], corner)
-        mean, scale = batch_stats(edge[1 : rows + 1], tile_mid, all_mid, 2 * b)
+        mean, scale, w = batch_stats(
+            edge[1 : rows + 1], all_mid, 2 * b, functools.partial(after_first, b)
+        )
         for view, link in zip((halo_row.at[b], halo_col.at[b], halo_cor.at[b]), links):
             left(view, link)
             arrived(view, link)
@@ -411,18 +474,6 @@
         prev = pltpu.roll(a, 1, 1).reshape(tall, mid)
         after = pltpu.roll(a, pitch - 1, 1).reshape(tall, mid)
         wide = jnp.concatenate([prev, a.reshape(tall, mid), after], axis=-1).astype(BF16)
-        if b == 0:
-            have_norms()
-            sums = jnp.sum(nc[...], axis=0)
-            base_sq = sums[0:1]
-            pc[me] = (
-                class_arrays[0]
-                + alpha[0] * unit_ratio(base_sq, sums[1:2]) * class_arrays[1]
-                + alpha[1] * unit_ratio(base_sq, sums[2:3]) * class_arrays[2]
-            ).astype(BF16)
-            have_class = share_parts(pc)
-            have_spatial()
-        w = rows_joined(ps[:, b])
         span = 3 * mid
         y = sum(
             lax.dot_general(
@@ -434,38 +485,48 @@
             for i in range(3)
         )
         y2s[...] = y.reshape(rows, pitch, mid)
-        mean, scale = batch_stats(y2s[...], tile_mid, all_mid, 2 * b + 1)
+        mean, scale, w = batch_stats(
+            y2s[...], all_mid, 2 * b + 1, functools.partial(after_second, b)
+        )
         gain = scale * gm_ref[b, 1:2]
         c = jax.nn.relu((y2s[...] - mean[None]) * gain[None] + sm_ref[b, 1:2][None])
-        if b == 0:
-            have_expand()
-        w = rows_joined(pe[:, b])
         y = lax.dot_general(
             c.reshape(flat, mid).astype(BF16), w, NT, preferred_element_type=F32
         )
         y3s[...] = y.reshape(rows, pitch, width)
-        mean, scale = batch_stats(y3s[...], tile_out, all_out, b)
+        mean, scale, w_reduce = batch_stats(
+            y3s[...], all_out, b, functools.partial(after_third, b)
+        )
         gain = scale * go_ref[b : b + 1]
         e = (y3s[...] - mean[None]) * gain[None] + so_ref[b : b + 1][None]
         xs[...] = jnp.where(inside, jax.nn.relu(xs[...].astype(F32) + e), 0.0).astype(BF16)
 
     final = xs[...]
-    pooled_parts[tile] = jnp.sum(final.astype(F32), axis=(0, 1), keepdims=True)[0]
-    have_pooled = share_tiles(pooled_parts)
+    pooled_parts[place, 0:1, :] = jnp.sum(final.astype(F32), axis=(0, 1), keepdims=True)[0]
+    pooled_parts[place, 1:2, :] = jnp.full((1, width), labels_ref[0].astype(F32))
+    have_pooled = share_all(pooled_parts)
     out_ref[...] = xs[:, 0:cols, :]
-    have_class()
+    have["class"]()
+    w = rows_joined(pc[...])
     have_pooled()
-    total = jnp.sum(pooled_parts[...], axis=0)
-    pooled = (total / (rows * cols * 4)).astype(BF16)
-    logits = jnp.dot(pooled, rows_joined(pc[...]), preferred_element_type=F32)
+    by_image = [
+        functools.reduce(jnp.add, [pooled_parts[i * tiles + t, 0:1, :] for t in range(tiles)])
+        for i in range(parts)
+    ]
+    pooled = (jnp.concatenate(by_image, axis=0) / (rows * cols * tiles)).astype(BF16)
+    wanted = jnp.concatenate([pooled_parts[i * tiles, 1:2, 0:1] for i in range(parts)], axis=0)
+    logits = jnp.dot(pooled, w, preferred_element_type=F32)
     summed = jnp.log(jnp.sum(jnp.exp(logits), axis=1, keepdims=True))
-    index = lax.broadcasted_iota(jnp.int32, logits.shape, 1)
-    picked = jnp.sum(jnp.where(index == labels_ref[0], logits, 0.0), axis=1, keepdims=True)
-    loss = jnp.broadcast_to(summed - picked, loss_ref.shape)
-    loss_ref[...] = loss
-    loss_parts[me] = loss
-    share_parts(loss_parts)()
-    mean_ref[...] = jnp.mean(loss_parts[...], axis=0)
+    index = lax.broadcasted_iota(jnp.int32, logits.shape, 1).astype(F32)
+    picked = jnp.sum(jnp.where(index == wanted, logits, 0.0), axis=1, keepdims=True)
+    losses = summed - picked
+    image = lax.broadcasted_iota(jnp.int32, losses.shape, 0)
+    loss_ref[...] = jnp.broadcast_to(
+        jnp.sum(jnp.where(image == me, losses, 0.0), axis=0, keepdims=True), loss_ref.shape
+    )
+    mean_ref[...] = jnp.broadcast_to(
+        jnp.sum(losses, axis=0, keepdims=True) / parts, mean_ref.shape
+    )
     for view, link in pending:
         left(view, link)
 
@@ -499,7 +560,7 @@
     ) + tuple(args[11:])
     vmem = pl.BlockSpec(memory_space=pltpu.VMEM)
     smem = pl.BlockSpec(memory_space=pltpu.SMEM)
-    links = 7 + 9 * blocks
+    links = 3 + 9 * blocks
     out, loss, mean_loss = pl.pallas_call(
         functools.partial(section_kernel, parts),
         out_shape=(
@@ -514,20 +575,17 @@
             pltpu.VMEM((rows + 2, pitch, mid), F32),
             pltpu.VMEM((rows, pitch, mid), F32),
             pltpu.VMEM((rows, pitch, width), F32),
-            pltpu.VMEM((parts, blocks, own_mid, width), BF16),
-            pltpu.VMEM((parts, blocks, own_mid, taps * mid), BF16),
-            pltpu.VMEM((parts, blocks, own_out, mid), BF16),
+            pltpu.VMEM((blocks, parts, own_mid, width), BF16),
+            pltpu.VMEM((blocks, parts, own_mid, taps * mid), BF16),
+            pltpu.VMEM((blocks, parts, own_out, mid), BF16),
             pltpu.VMEM((parts, own_feat, classes), BF16),
             pltpu.VMEM((parts, 3, classes), F32),
-            pltpu.VMEM((2 * blocks, 4, 2, mid), F32),
-            pltpu.VMEM((blocks, 4, 2, width), F32),
-            pltpu.VMEM((2 * blocks, parts, 2, mid), F32),
-            pltpu.VMEM((blocks, parts, 2, width), F32),
+            pltpu.VMEM((2 * blocks, parts * 4, 2, mid), F32),
+            pltpu.VMEM((blocks, parts * 4, 2, width), F32),
             pltpu.VMEM((blocks, pitch, mid), F32),
             pltpu.VMEM((blocks, rows, 8, mid), F32),
             pltpu.VMEM((blocks, 8, mid), F32),
-            pltpu.VMEM((4, 1, width), F32),
-            pltpu.VMEM((parts, 1, 128), F32),
+            pltpu.VMEM((parts * 4, 2, width), F32),
             pltpu.SemaphoreType.DMA((links,)),
             pltpu.SemaphoreType.DMA((links,)),
         ],

time: 103 us -> 81.8 us (0.79)
  Pallas kernels: 96.7 us -> 75.5 us
    pallas_call x1, Pallas kernels: 96.7 us -> 75.5 us  [fused(): pl.pallas_call(functools.partial(section_kernel, parts), out_shape=(jax.S...]
where the time goes in v2:
time: 81.8 us; the launch traced here: 81.6 us
  Pallas kernels  75.5 us (92%)
  between operations  3.63 us (4%)
  local copies, waits for them, and re-layouts  2.46 us (3%)
    pallas_call x1, Pallas kernels, fused(): pl.pallas_call(functools.partial(section_kernel, parts), out_shape=(jax.S...  75.5 us
    unnamed x5, local copies, waits for them, and re-layouts  2.46 us

profile of v2, /device:TPU:0, one launch (start us, length us, event | category | flops | bytes accessed | tf_op | source)
XLA Modules:
  0.0 81.6 jit_solution(4717178038126029856)
XLA Ops:
  1.3 75.5 %shard_map.166 = (bf16[28,28,256]{2,1,0:T(8,128)(2,1)}, f32[1,128]{1,0:T(1,128)}, f32[1,128]{1,0:T(1,128)}) custom-call(bf16[28,28,256]{2,1,0:T(8,128)(2,1)} %bitcast.16, s32[1]{0:T(128)S(6)} %copy.21.labels_ref, s32[2]{0:T(128)} %grid_ref.1, bf16[3,8,256]{2,1,0:T(8,128)(2,1)} %bitcast.23, bf16[3,9,8,64]{3,2,1,0:T(8,128)(2,1)} %bitcast.19, ...), custom_call_target="tpu_custom_call" | custom-call | tf_op jit(solution)/shard_map/pallas_call | solution.py:564
  76.8 0.0 copy-start.1
  76.8 1.8 %copy.22 = bf16[1,28,28,256]{3,2,1,0:T(8,128)(2,1)} copy(bf16[1,28,28,256]{3,2,1,0:T(8,128)(2,1)} %bitcast.17) | data formatting | bytes 802816
  78.6 0.0 copy-done.1
  78.6 0.0 copy-start
  78.7 0.6 copy-done
Async XLA Ops:
  76.8 1.8 %copy-start.1 = (f32[1,128]{1,0:T(1,128)S(1)}, f32[1,128]{1,0:T(1,128)}, u32[]{:S(2)}) copy-start(f32[1,128]{1,0:T(1,128)} %get-tuple-element.7) | copy-start | bytes 1540
  78.6 0.7 copy-start

commit v3 on v2

--- a/solution.py
+++ b/solution.py
@@ -232,8 +232,22 @@
     beside = {"sx": 1 - my_x}
     corner = {"sy": 1 - my_y, "sx": 1 - my_x}
 
+    sides_y, sides_x = (my_y, 1 - my_y), (my_x, 1 - my_x)
+
     def peer(d):
-        return {"dp": lax.rem(me + d, parts)}
+        other = me + d
+        return {"dp": jnp.where(other >= parts, other - parts, other)}
+
+    def each_device(act):
+        for k in range(1, tiles):
+            act({"sy": sides_y[k // 2], "sx": sides_x[k % 2]})
+
+        def step(d, carry):
+            for k in range(tiles):
+                act({**peer(d), "sy": sides_y[k // 2], "sx": sides_x[k % 2]})
+            return carry
+
+        lax.fori_loop(1, parts, step, 0)
 
     def each_part(act):
         def step(d, carry):
@@ -278,17 +292,7 @@
         link = channel()
         own = buffer.at[place]
 
-        def step(d, carry):
-            other = lax.rem(place + d, devices)
-            device = {
-                "dp": lax.div(other, tiles),
-                "sy": lax.rem(lax.div(other, 2), 2),
-                "sx": lax.rem(other, 2),
-            }
-            push(own, own, link, device)
-            return carry
-
-        lax.fori_loop(1, devices, step, 0)
+        each_device(lambda device: push(own, own, link, device))
         view = buffer.at[pl.ds(0, devices - 1)]
         pending.append((view, link))
         return lambda: arrived(view, link)
@@ -298,18 +302,7 @@
     def greet(device):
         pl.semaphore_signal(barrier, inc=1, device_id=device, device_id_type=pl.DeviceIdType.MESH)
 
-    def greet_step(d, carry):
-        other = lax.rem(place + d, devices)
-        greet(
-            {
-                "dp": lax.div(other, tiles),
-                "sy": lax.rem(lax.div(other, 2), 2),
-                "sx": lax.rem(other, 2),
-            }
-        )
-        return carry
-
-    lax.fori_loop(1, devices, greet_step, 0)
+    each_device(greet)
 
     alpha = [(2.0 * grid_ref[k].astype(F32) + (1.0 - GRID)) * (1.0 / GRID) for k in range(2)]
 
@@ -380,9 +373,11 @@
     xs[...] = jnp.zeros_like(xs)
     xs[:, 0:cols, :] = x_ref[...]
 
-    inside = lax.broadcasted_iota(jnp.int32, (rows, pitch, 1), 1) < cols
-    edge_row = lax.broadcasted_iota(jnp.int32, (rows + 2, pitch, 1), 0)
-    edge_col = lax.broadcasted_iota(jnp.int32, (rows + 2, pitch, 1), 1)
+    def inside(depth):
+        return lax.broadcasted_iota(jnp.int32, (1, pitch, depth), 1) < cols
+
+    edge_row = lax.broadcasted_iota(jnp.int32, (rows + 2, 1, mid), 0)
+    edge_col = lax.broadcasted_iota(jnp.int32, (1, pitch, mid), 1)
     far_row = jnp.where(my_y == 0, rows + 1, 0)
     far_col = jnp.where(my_x == 0, cols, pitch - 1)
     valid = ((edge_row >= 1) & (edge_row <= rows) | (edge_row == far_row)) & (
@@ -393,10 +388,11 @@
     slot = far_col - last
 
     def local_stats(value):
-        masked = jnp.where(inside, value, 0.0)
-        mean = jnp.sum(masked, axis=(0, 1), keepdims=True)[0] / (rows * cols)
-        centred = jnp.where(inside, value - mean[None], 0.0)
-        return mean, jnp.sum(centred * centred, axis=(0, 1), keepdims=True)[0] / (rows * cols)
+        origin = value[0:1, 0:1, :]
+        gap = jnp.where(inside(value.shape[-1]), value - origin, 0.0)
+        offset = jnp.sum(gap, axis=(0, 1), keepdims=True)[0] / (rows * cols)
+        square = jnp.sum(gap * gap, axis=(0, 1), keepdims=True)[0] / (rows * cols)
+        return origin[0] + offset, jnp.maximum(square - offset * offset, 0.0)
 
     def pooled_stats(buffer, r):
         means, spreads = buffer[r, :, 0:1, :], buffer[r, :, 1:2, :]
@@ -455,12 +451,12 @@
             left(view, link)
             arrived(view, link)
         shifted = pltpu.roll(halo_col[b].reshape(rows * 8, mid), 4, 0).reshape(rows, 8, mid)
-        lane8 = lax.broadcasted_iota(jnp.int32, (rows, 8, 1), 1)
+        lane8 = lax.broadcasted_iota(jnp.int32, (1, 8, mid), 1)
         edge[1 : rows + 1, last:pitch, :] = jnp.where(
             lane8 == slot, shifted, edge[1 : rows + 1, last:pitch, :]
         )
         edge[far_row] = halo_row[b]
-        end8 = lax.broadcasted_iota(jnp.int32, (8, 1), 0)
+        end8 = lax.broadcasted_iota(jnp.int32, (8, mid), 0)
         edge[far_row, last:pitch, :] = jnp.where(
             end8 == slot, pltpu.roll(halo_cor[b], 4, 0), halo_row[b, last:pitch, :]
         )
@@ -499,10 +495,10 @@
         )
         gain = scale * go_ref[b : b + 1]
         e = (y3s[...] - mean[None]) * gain[None] + so_ref[b : b + 1][None]
-        xs[...] = jnp.where(inside, jax.nn.relu(xs[...].astype(F32) + e), 0.0).astype(BF16)
-
-    final = xs[...]
-    pooled_parts[place, 0:1, :] = jnp.sum(final.astype(F32), axis=(0, 1), keepdims=True)[0]
+        xs[...] = jax.nn.relu(xs[...].astype(F32) + e).astype(BF16)
+
+    final = jnp.where(inside(width), xs[...].astype(F32), 0.0)
+    pooled_parts[place, 0:1, :] = jnp.sum(final, axis=(0, 1), keepdims=True)[0]
     pooled_parts[place, 1:2, :] = jnp.full((1, width), labels_ref[0].astype(F32))
     have_pooled = share_all(pooled_parts)
     out_ref[...] = xs[:, 0:cols, :]

time: 81.8 us -> 80.3 us (0.982)
  Pallas kernels: 75.5 us -> 74.1 us
    pallas_call x1, Pallas kernels: 75.5 us -> 74.1 us  [fused(): pl.pallas_call(functools.partial(section_kernel, parts), out_shape=(jax.S...]
where the time goes in v3:
time: 80.3 us; the launch traced here: 80.1 us
  Pallas kernels  74.1 us (92%)
  between operations  3.63 us (5%)
  local copies, waits for them, and re-layouts  2.46 us (3%)
    pallas_call x1, Pallas kernels, fused(): pl.pallas_call(functools.partial(section_kernel, parts), out_shape=(jax.S...  74.1 us
    unnamed x5, local copies, waits for them, and re-layouts  2.46 us

profile of v3, /device:TPU:0, one launch (start us, length us, event | category | flops | bytes accessed | tf_op | source)
XLA Modules:
  0.0 80.1 jit_solution(6410726639704726532)
XLA Ops:
  1.3 74.1 %shard_map.166 = (bf16[28,28,256]{2,1,0:T(8,128)(2,1)}, f32[1,128]{1,0:T(1,128)}, f32[1,128]{1,0:T(1,128)}) custom-call(bf16[28,28,256]{2,1,0:T(8,128)(2,1)} %bitcast.16, s32[1]{0:T(128)S(6)} %copy.21.labels_ref, s32[2]{0:T(128)} %grid_ref.1, bf16[3,8,256]{2,1,0:T(8,128)(2,1)} %bitcast.23, bf16[3,9,8,64]{3,2,1,0:T(8,128)(2,1)} %bitcast.19, ...), custom_call_target="tpu_custom_call" | custom-call | tf_op jit(solution)/shard_map/pallas_call | solution.py:560
  75.3 0.0 copy-start.1
  75.4 1.8 %copy.22 = bf16[1,28,28,256]{3,2,1,0:T(8,128)(2,1)} copy(bf16[1,28,28,256]{3,2,1,0:T(8,128)(2,1)} %bitcast.17) | data formatting | bytes 802816
  77.2 0.0 copy-done.1
  77.2 0.0 copy-start
  77.2 0.6 copy-done
Async XLA Ops:
  75.3 1.8 %copy-start.1 = (f32[1,128]{1,0:T(1,128)S(1)}, f32[1,128]{1,0:T(1,128)}, u32[]{:S(2)}) copy-start(f32[1,128]{1,0:T(1,128)} %get-tuple-element.7) | copy-start | bytes 1540
  77.2 0.7 copy-start
